TPU v7x, 128 devices: a whole 4x4x4 slice. The times are simulated.
128 devices in a mesh: obl: 16 (over y, z), scn: 8 (over x, core).
Axes of the slice: x: 4, y: 4, z: 4, core: 2. Of those that a mesh axis runs over, the one named last changes fastest.
Arguments:
- factors: bfloat16 [32768, 128], P('scn'), may hold values from -6 to 6
- idiosyncratic: bfloat16 [32768, 32768], P('obl', 'scn'), may hold values from -6 to 6
- loadings: bfloat16 [32768, 128], P('obl'), may hold values from -0.375 to 0.375
- rating: int32 [32768], P('obl'), may hold values from 0 to 15
- barrier: float32 [16], replicated, may hold values from 1 to 3
- loss_given: float32 [32768], P('obl'), may hold values from 0.2 to 0.9
- sector: int32 [32768], P('obl'), may hold values from 0 to 15, as said below
- allowed: int32 [256, 16], replicated, may hold values from 0 to 1, as said below
- holdings: float32 [32768, 256], P('obl'), may hold values from 0.1 to 10
Outputs:
- positions: float32 [32768, 256], P('obl')
- shortfall: float32 [2, 256], replicated
Inputs may be any that keep to these rules, and one draw needn't show every extreme that they name: Each sector holds exactly 2048 obligors. `allowed`: every mandate allows at least one sector.
All inputs are finite; a program needn't handle non-finite values.
Results may differ from a plain program's by a relative error of at most 0.0003.
Values may be sent and summed in bfloat16 or wider, within the bound.
No kernel may reach another device: no remote copies, remote signals or barrier semaphores. Data moves between devices by JAX's collectives and lax.ppermute only.
A program may use at most 128 MiB of HBM per device.

v0:
```python
import functools
import jax
import jax.numpy as jnp
from jax import lax
from jax.sharding import Mesh
from jax.sharding import PartitionSpec as P

STEPS = 2
OBL = ("obl_0", "obl_1")
IDIO_SCALE = 0.8
SHARP = 2.0
LEVEL = 0.99
QUANTILE = 2.326
SMOOTH = 0.5
EPSILON = 1e-06
STEP_RATE = 8.0


def one_axis_at_a_time(array, axes):
    return functools.reduce(lax.psum, axes, array)


def copy_for_each(array, axis):
    devices = lax.axis_size(axis)
    return lax.all_to_all(
        jnp.broadcast_to(array[None], (devices, *array.shape)), axis, 0, 0, tiled=True
    )


def over_copies(array, axis):
    everything = copy_for_each(array, axis)
    return jnp.sum(everything, axis=0)


def together(arrays, axis):
    vector, at, outs = (jnp.concatenate([a.reshape(-1) for a in arrays]), 0, [])
    running = over_copies(vector, axis)
    for a in arrays:
        outs.append(running[at : at + a.size].reshape(a.shape))
        at += a.size
    return tuple(outs)


def filled_up(lines, devices):
    spare = -len(lines) % devices
    return jnp.pad(lines, [(0, spare)] + [(0, 0)] * (lines.ndim - 1))


def total_of(array, axis):
    lines = array.reshape(-1, *array.shape[1:][-1:])
    own = lax.psum_scatter(
        filled_up(lines, lax.axis_size(axis)), axis, scatter_dimension=0, tiled=True
    )
    whole = lax.all_gather(own, axis).reshape(-1, *lines.shape[1:])
    return lax.slice_in_dim(whole, 0, len(lines)).reshape(array.shape)


def tail_terms(losses, center, spread, tail_scale):
    deviation = jnp.sqrt(spread + EPSILON)
    thresh = center + QUANTILE * deviation
    smooth_width = SMOOTH * deviation
    scaled = (losses - thresh) / smooth_width
    tail_weight = (jax.nn.sigmoid(scaled) * tail_scale).astype(jnp.bfloat16)
    return (scaled, thresh, smooth_width, tail_weight)


def on_device(
    factors, idiosyncratic, loadings, rating, barrier, loss_given, sector, allowed, holdings
):
    obl_dev = idiosyncratic.shape[0]
    scn_dev = idiosyncratic.shape[1]
    obligors = obl_dev * lax.axis_size(OBL)
    scenarios = scn_dev * lax.axis_size("scn")
    tail_scale = 1.0 / ((1.0 - LEVEL) * scenarios)
    sector_hot = (sector[:, None] == jnp.arange(allowed.shape[1])[None, :]).astype(jnp.float32)
    eligible = lax.dot_general(
        sector_hot,
        allowed.astype(jnp.float32),
        (((1,), (1,)), ((), ())),
        precision=lax.Precision.HIGHEST,
    )
    rating_hot = (rating[:, None] == jnp.arange(barrier.shape[0])[None, :]).astype(jnp.float32)
    barrier_rows = jnp.dot(rating_hot, barrier, precision=lax.Precision.HIGHEST)
    systematic = lax.dot_general(
        loadings, factors, (((1,), (1,)), ((), ())), preferred_element_type=jnp.float32
    )
    latent = systematic + IDIO_SCALE * idiosyncratic.astype(jnp.float32)
    default_prob = jax.nn.sigmoid((latent - barrier_rows[:, None]) * SHARP).astype(jnp.bfloat16)
    weighted = eligible * holdings
    totals = one_axis_at_a_time(jnp.sum(weighted, 0), OBL)
    positions = obligors * weighted / totals
    results = []
    for iteration in range(STEPS):
        exposure = (loss_given[:, None] * positions / obligors).astype(jnp.bfloat16)
        partial_value = lax.dot_general(
            default_prob, exposure, (((0,), (0,)), ((), ())), preferred_element_type=jnp.float32
        )
        losses = lax.psum(partial_value, OBL)
        first, second = together((jnp.sum(losses, 0), jnp.sum(losses * losses, 0)), "scn")
        center = first / scenarios
        spread = second / scenarios - center * center
        scaled, thresh, smooth_width, tail_weight = tail_terms(losses, center, spread, tail_scale)
        tail_sum = over_copies(jnp.sum(jax.nn.softplus(scaled), 0), "scn")
        results.append(thresh + smooth_width * (tail_sum * tail_scale))
        gradient = jnp.dot(default_prob, tail_weight, preferred_element_type=jnp.float32)
        gradient = total_of(gradient, "scn")
        gradient = loss_given[:, None] * eligible * gradient
        unnorm = positions * jnp.exp(-STEP_RATE * gradient)
        totals = one_axis_at_a_time(jnp.sum(unnorm, 0), OBL)
        positions = obligors * unnorm / totals
    return (positions, jnp.stack(results))


def solution(mesh):
    finer = Mesh(mesh.devices.reshape(4, 4, mesh.shape["scn"]), ("obl_0", "obl_1", "scn"))
    in_specs = (
        P("scn", None),
        P(OBL, "scn"),
        P(OBL, None),
        P(OBL),
        P(),
        P(OBL),
        P(OBL),
        P(),
        P(OBL, None),
    )
    out_specs = (P(OBL, None), P())
    return jax.shard_map(
        on_device, mesh=finer, in_specs=in_specs, out_specs=out_specs, check_vma=False
    )
```

profile of v0, /device:TPU:0, one launch (start us, length us, event | category | flops | bytes accessed | tf_op | source)
XLA Modules:
  0.0 505.9 jit_solution(1851774986560804028)
XLA Ops:
  9.9 10.9 %psum.56 = f32[256]{0:T(256)S(1)} all-reduce(f32[256]{0:T(256)S(1)} %get-tuple-element.14), channel_id=1, replica_groups=mesh['obl_0'=4,'obl_1'=4,'scn'=8] {'obl_0'}, use_global_device_ids=true, to_apply=%region_1.0 | all-reduce | flops 256 | bytes 2048 | tf_op jit(solution)/shard_map/psum | solution.py:20
  20.8 11.8 %psum.57 = f32[256]{0:T(256)S(1)} all-reduce(f32[256]{0:T(256)S(1)} %psum.56), channel_id=1, replica_groups=mesh['obl_0'=4,'obl_1'=4,'scn'=8] {'obl_1'}, use_global_device_ids=true, to_apply=%region_2.0 | all-reduce | flops 256 | bytes 2048 | tf_op jit(solution)/shard_map/psum | solution.py:20
  33.3 16.5 %divide_convert_fusion = bf16[2048,4096]{1,0:T(8,128)(2,1)} fusion(bf16[2048,4096]{1,0:T(8,128)(2,1)} %param.10, f32[2048]{0:T(1024)S(1)} %bitcast.14, bf16[2048,128]{1,0:T(8,128)(2,1)} %param.11, bf16[4096,128]{1,0:T(8,128)(2,1)S(1)} %copy-done), kind=kOutput, calls=%fused_computation | convolution fusion | flops 2222981120 | bytes 35135488 | tf_op jit(solution)/shard_map/dot_general | solution.py:84
  49.8 13.6 %fusion.8 = f32[4096,256]{1,0:T(8,128)} fusion(bf16[2048,4096]{1,0:T(8,128)(2,1)} %divide_convert_fusion, f32[2048]{0:T(1024)S(1)} %copy-done.2, f32[256]{0:T(256)S(1)} %psum.57, f32[2048,256]{1,0:T(8,128)S(1)} %get-tuple-element.15, f32[2048,256]{1,0:T(8,128)} %param.17), kind=kOutput, calls=%fused_computation.24 | convolution fusion | flops 4298113024 | bytes 25175040 | tf_op jit(solution)/shard_map/dot_general | solution.py:95
  63.5 100.8 %all-reduce.3.cloned.1.call-done = f32[4096,256]{1,0:T(8,128)} async-done(((f32[4096,256]{1,0:T(8,128)}), f32[4096,256]{1,0:T(8,128)}) %all-reduce.3.cloned.1.call-update) | async-done | bytes 4194320 | tf_op jit(solution)/shard_map/psum | solution.py:98
  167.0 9.4 %all_to_all.24 = f32[8,1,512]{2,1,0:T(1,128)S(1)} all-to-all(f32[8,1,512]{2,1,0:T(1,128)S(1)} %broadcast_in_dim.8), channel_id=1, replica_groups=mesh['obl_0'=4,'obl_1'=4,'scn'=8] {'scn'}, dimensions={0} | all-to-all | bytes 32768 | tf_op jit(solution)/shard_map/all_to_all | solution.py:25
  176.5 13.1 %fusion.2 = f32[2048,256]{1,0:T(8,128)} fusion(bf16[2048,4096]{1,0:T(8,128)(2,1)} %divide_convert_fusion, f32[4096,256]{1,0:T(8,128)} %all-reduce.3.cloned.1.call-done, f32[256]{0:T(256)S(1)} %broadcast_multiply_fusion.1, f32[256]{0:T(256)S(1)} %get-tuple-element.12), kind=kOutput, calls=%fused_computation.11 | convolution fusion | flops 4302307328 | bytes 23070720 | tf_op jit(solution)/shard_map/dot_general | solution.py:105
  189.7 31.7 %reduce-scatter.3.cloned.1.call-done = f32[256,256]{1,0:T(8,128)} async-done(((f32[2048,256]{1,0:T(8,128)}), f32[256,256]{1,0:T(8,128)}) %reduce-scatter.3.cloned.1.call-update) | async-done | bytes 262160 | tf_op jit(solution)/shard_map/reduce_scatter | solution.py:51
  221.5 25.9 %all-gather.5.cloned.1.call-done = f32[2048,256]{1,0:T(8,128)} async-done(((f32[256,256]{1,0:T(8,128)}), f32[2048,256]{1,0:T(8,128)}) %all-gather.5.cloned.1.call-update) | async-done | bytes 2097168 | tf_op jit(solution)/shard_map/all_gather | solution.py:54
  247.4 4.3 fusion.31
  251.7 10.4 %psum.59 = f32[256]{0:T(256)S(1)} all-reduce(f32[256]{0:T(256)S(1)} %get-tuple-element.10), channel_id=1, replica_groups=mesh['obl_0'=4,'obl_1'=4,'scn'=8] {'obl_0'}, use_global_device_ids=true, to_apply=%region_9.10 | all-reduce | flops 256 | bytes 2048 | tf_op jit(solution)/shard_map/psum | solution.py:20
  262.1 10.7 %psum.60 = f32[256]{0:T(256)S(1)} all-reduce(f32[256]{0:T(256)S(1)} %psum.59), channel_id=1, replica_groups=mesh['obl_0'=4,'obl_1'=4,'scn'=8] {'obl_1'}, use_global_device_ids=true, to_apply=%region_10.11 | all-reduce | flops 256 | bytes 2048 | tf_op jit(solution)/shard_map/psum | solution.py:20
  272.8 13.6 %fusion.9 = f32[4096,256]{1,0:T(8,128)} fusion(bf16[2048,4096]{1,0:T(8,128)(2,1)} %divide_convert_fusion, f32[2048]{0:T(1024)S(1)} %copy-done.2, f32[2048,256]{1,0:T(8,128)} %get-tuple-element.11, f32[256]{0:T(256)S(1)} %psum.60), kind=kOutput, calls=%fused_computation.25 | convolution fusion | flops 4297588736 | bytes 23077888 | tf_op jit(solution)/shard_map/dot_general | solution.py:95
  286.6 99.7 %all-reduce.5.cloned.1.call-done = f32[4096,256]{1,0:T(8,128)} async-done(((f32[4096,256]{1,0:T(8,128)}), f32[4096,256]{1,0:T(8,128)}) %all-reduce.5.cloned.1.call-update) | async-done | bytes 4194320 | tf_op jit(solution)/shard_map/psum | solution.py:98
  389.1 9.4 %all_to_all.25 = f32[8,1,512]{2,1,0:T(1,128)S(1)} all-to-all(f32[8,1,512]{2,1,0:T(1,128)S(1)} %broadcast_in_dim.9), channel_id=1, replica_groups=mesh['obl_0'=4,'obl_1'=4,'scn'=8] {'scn'}, dimensions={0} | all-to-all | bytes 32768 | tf_op jit(solution)/shard_map/all_to_all | solution.py:25
  398.5 13.2 %fusion.3 = f32[2048,256]{1,0:T(8,128)} fusion(bf16[2048,4096]{1,0:T(8,128)(2,1)} %divide_convert_fusion, f32[4096,256]{1,0:T(8,128)} %all-reduce.5.cloned.1.call-done, f32[256]{0:T(256)S(1)} %broadcast_multiply_fusion, f32[256]{0:T(256)S(1)} %get-tuple-element.8), kind=kOutput, calls=%fused_computation.12 | convolution fusion | flops 4302307328 | bytes 23070720 | tf_op jit(solution)/shard_map/dot_general | solution.py:105
  411.8 31.8 %reduce-scatter.5.cloned.1.call-done = f32[256,256]{1,0:T(8,128)} async-done(((f32[2048,256]{1,0:T(8,128)}), f32[256,256]{1,0:T(8,128)}) %reduce-scatter.5.cloned.1.call-update) | async-done | bytes 262160 | tf_op jit(solution)/shard_map/reduce_scatter | solution.py:51
  443.6 4.8 fusion
  448.4 7.7 %all_to_all.26 = f32[8,1,256]{2,1,0:T(1,128)S(1)} all-to-all(f32[8,1,256]{2,1,0:T(1,128)S(1)} %broadcast_in_dim.10), channel_id=1, replica_groups=mesh['obl_0'=4,'obl_1'=4,'scn'=8] {'scn'}, dimensions={0} | all-to-all | bytes 16384 | tf_op jit(solution)/shard_map/all_to_all | solution.py:25
  456.1 4.8 fusion.1
  464.8 5.2 %all-to-all-done.3 = f32[8,1,256]{2,1,0:T(1,128)S(1)} async-done(((f32[8,1,256]{2,1,0:T(1,128)}), f32[8,1,256]{2,1,0:T(1,128)S(1)}, u32[]{:S(2)}, u32[]{:S(2)}) %all-to-all-start.3) | async-done | bytes 8224 | tf_op jit(solution)/shard_map/all_to_all | solution.py:25
  470.6 4.3 fusion.30
  474.9 10.4 %psum.62 = f32[256]{0:T(256)S(1)} all-reduce(f32[256]{0:T(256)S(1)} %get-tuple-element.6), channel_id=1, replica_groups=mesh['obl_0'=4,'obl_1'=4,'scn'=8] {'obl_0'}, use_global_device_ids=true, to_apply=%region_17.18 | all-reduce | flops 256 | bytes 2048 | tf_op jit(solution)/shard_map/psum | solution.py:20
  485.4 10.7 %psum.63 = f32[256]{0:T(256)S(1)} all-reduce(f32[256]{0:T(256)S(1)} %psum.62), channel_id=1, replica_groups=mesh['obl_0'=4,'obl_1'=4,'scn'=8] {'obl_1'}, use_global_device_ids=true, to_apply=%region_18.19 | all-reduce | flops 256 | bytes 2048 | tf_op jit(solution)/shard_map/psum | solution.py:20
  (46 shorter events, 17.2 us)
Async XLA Ops:
  7.2 26.1 %copy-start = (bf16[4096,128]{1,0:T(8,128)(2,1)S(1)}, bf16[4096,128]{1,0:T(8,128)(2,1)}, u32[]{:S(2)}) copy-start(bf16[4096,128]{1,0:T(8,128)(2,1)} %param.9) | copy-start | bytes 3145732
  7.2 25.3 %copy-start.4 = (f32[16]{0:T(128)S(1)}, f32[16]{0:T(128)}, u32[]{:S(2)}) copy-start(f32[16]{0:T(128)} %param.13) | copy-start | bytes 196
  7.2 25.3 %copy-start.3 = (s32[2048]{0:T(1024)S(1)}, s32[2048]{0:T(1024)}, u32[]{:S(2)}) copy-start(s32[2048]{0:T(1024)} %param.12) | copy-start | bytes 24580
  7.2 157.1 %all-reduce.3.cloned.1.call-start = ((), (), s32[]{:S(2)}) async-start(), calls=%async_computation.6 | async-start | bytes 8388608 | tf_op jit(solution)/shard_map/psum | solution.py:98
  33.2 16.5 %copy-start.2 = (f32[2048]{0:T(1024)S(1)}, f32[2048]{0:T(1024)}, u32[]{:S(2)}) copy-start(f32[2048]{0:T(1024)} %param.14) | copy-start | bytes 24580
  63.4 158.0 %reduce-scatter.3.cloned.1.call-start = ((), (), s32[]{:S(2)}) async-start(), calls=%async_computation.7 | async-start | bytes 2359296 | tf_op jit(solution)/shard_map/reduce_scatter | solution.py:51
  189.7 57.7 %all-gather.5.cloned.1.call-start = ((), (), s32[]{:S(2)}) async-start(), calls=%async_computation.10 | async-start | bytes 2359296 | tf_op jit(solution)/shard_map/all_gather | solution.py:54
  221.5 164.8 %all-reduce.5.cloned.1.call-start = ((), (), s32[]{:S(2)}) async-start(), calls=%async_computation.8 | async-start | bytes 8388608 | tf_op jit(solution)/shard_map/psum | solution.py:98
  286.4 157.3 %reduce-scatter.5.cloned.1.call-start = ((), (), s32[]{:S(2)}) async-start(), calls=%async_computation.9 | async-start | bytes 2359296 | tf_op jit(solution)/shard_map/reduce_scatter | solution.py:51
  411.8 58.9 %all-gather.7.cloned.1.call-start = ((), (), s32[]{:S(2)}) async-start(), calls=%async_computation.11 | async-start | bytes 2359296 | tf_op jit(solution)/shard_map/all_gather | solution.py:54
  461.5 8.5 %all-to-all-start.3 = ((f32[8,1,256]{2,1,0:T(1,128)}), f32[8,1,256]{2,1,0:T(1,128)S(1)}, u32[]{:S(2)}, u32[]{:S(2)}) async-start(f32[8,1,256]{2,1,0:T(1,128)} %broadcast_in_dim.11), calls=%async_computation.5 | async-start | bytes 16384 | tf_op jit(solution)/shard_map/all_to_all | solution.py:25
  470.6 28.5 %copy-start.1 = (bf16[4096,128]{1,0:T(8,128)(2,1)S(1)}, bf16[4096,128]{1,0:T(8,128)(2,1)}, u32[]{:S(2)}) copy-start(bf16[4096,128]{1,0:T(8,128)(2,1)} %param.9) | copy-start | bytes 3145732
Sparse Core Ops, SparseCore 0:
  63.5 100.6 all-reduce.2
  189.8 31.5 reduce-scatter.2
  223.2 24.1 all-gather.4
  286.5 99.7 all-reduce.4
  411.9 31.6 reduce-scatter.4
  445.2 24.0 all-gather.6
where the time goes:
time: 507 us; the launch traced here: 506 us
  waiting for transfers between devices  295 us (58%)
  blocking collectives  91.3 us (18%)
  matrix products  73.4 us (14%)
  other arithmetic  27.4 us (5%)
  between operations  14.2 us (3%)
    psum x2, waiting for transfers between devices, on_device(): losses = lax.psum(partial_value, OBL)  200 us
    psum x6, blocking collectives, one_axis_at_a_time(): return functools.reduce(lax.psum, axes, array)  64.8 us
    reduce_scatter x2, waiting for transfers between devices, total_of(): lax.psum_scatter(filled_up(lines, lax.axis_size(axis)), axis, scatter_dim...  63.5 us
    dot_general x2, matrix products, on_device(): lax.dot_general(default_prob, exposure, (((0,), (0,)), ((), ())), preferr...  27.2 us
    all_to_all x3, blocking collectives, copy_for_each(): lax.all_to_all(jnp.broadcast_to(array[None], (devices, *array.shape)), ax...  26.5 us
    dot_general x2, matrix products, on_device(): jnp.dot(default_prob, tail_weight, preferred_element_type=jnp.float32)  26.4 us
    all_gather x2, waiting for transfers between devices, total_of(): whole = lax.all_gather(own, axis).reshape(-1, *lines.shape[1:])  25.9 us
    dot_general x1, matrix products, on_device(): lax.dot_general(loadings, factors, (((1,), (1,)), ((), ())), preferred_el...  16.5 us
  transfers between devices with their start and end apart: 7, of which 6 were waited for; matrix products, arithmetic and copies ran while one was open for 2% of the time, Pallas kernels for 0%

commit v1 on v0

--- a/solution.py
+++ b/solution.py
@@ -95,7 +95,9 @@
         partial_value = lax.dot_general(
             default_prob, exposure, (((0,), (0,)), ((), ())), preferred_element_type=jnp.float32
         )
-        losses = lax.psum(partial_value, OBL)
+        losses = partial_value
+        for mesh_axis in ("obl_0", "obl_1"):
+            losses = lax.psum(losses, mesh_axis)
         first, second = together((jnp.sum(losses, 0), jnp.sum(losses * losses, 0)), "scn")
         center = first / scenarios
         spread = second / scenarios - center * center

time: 507 us -> 675 us (1.33)
  waiting for transfers between devices: 295 us -> 463 us
    psum x2 -> x4, waiting for transfers between devices: 200 us -> 369 us  [on_device(): losses = lax.psum(losses, mesh_axis)]
  transfers between devices with their start and end apart: 7 -> 9, of which waited for: 6 -> 8; matrix products, arithmetic and copies ran while one was open for 2% -> 2% of each run, Pallas kernels for 0% -> 0%
where the time goes in v1:
time: 675 us; the launch traced here: 674 us
  waiting for transfers between devices  463 us (69%)
  blocking collectives  91.3 us (14%)
  matrix products  73.4 us (11%)
  other arithmetic  27.4 us (4%)
  between operations  14.2 us (2%)
    psum x4, waiting for transfers between devices, on_device(): losses = lax.psum(losses, mesh_axis)  369 us
    psum x6, blocking collectives, one_axis_at_a_time(): return functools.reduce(lax.psum, axes, array)  64.8 us
    reduce_scatter x2, waiting for transfers between devices, total_of(): lax.psum_scatter(filled_up(lines, lax.axis_size(axis)), axis, scatter_dim...  63.8 us
    dot_general x2, matrix products, on_device(): lax.dot_general(default_prob, exposure, (((0,), (0,)), ((), ())), preferr...  27.1 us
    all_to_all x3, blocking collectives, copy_for_each(): lax.all_to_all(jnp.broadcast_to(array[None], (devices, *array.shape)), ax...  26.5 us
    dot_general x2, matrix products, on_device(): jnp.dot(default_prob, tail_weight, preferred_element_type=jnp.float32)  26.4 us
    all_gather x2, waiting for transfers between devices, total_of(): whole = lax.all_gather(own, axis).reshape(-1, *lines.shape[1:])  25.5 us
    dot_general x1, matrix products, on_device(): lax.dot_general(loadings, factors, (((1,), (1,)), ((), ())), preferred_el...  16.5 us
  transfers between devices with their start and end apart: 9, of which 8 were waited for; matrix products, arithmetic and copies ran while one was open for 2% of the time, Pallas kernels for 0%

profile of v1, /device:TPU:0, one launch (start us, length us, event | category | flops | bytes accessed | tf_op | source)
XLA Modules:
  0.0 674.1 jit_solution(10769971168835517912)
XLA Ops:
  9.9 10.9 %psum.70 = f32[256]{0:T(256)S(1)} all-reduce(f32[256]{0:T(256)S(1)} %get-tuple-element.14), channel_id=1, replica_groups=mesh['obl_0'=4,'obl_1'=4,'scn'=8] {'obl_0'}, use_global_device_ids=true, to_apply=%region_1.0 | all-reduce | flops 256 | bytes 2048 | tf_op jit(solution)/shard_map/psum | solution.py:20
  20.8 11.8 %psum.71 = f32[256]{0:T(256)S(1)} all-reduce(f32[256]{0:T(256)S(1)} %psum.70), channel_id=1, replica_groups=mesh['obl_0'=4,'obl_1'=4,'scn'=8] {'obl_1'}, use_global_device_ids=true, to_apply=%region_2.0 | all-reduce | flops 256 | bytes 2048 | tf_op jit(solution)/shard_map/psum | solution.py:20
  33.3 16.5 %divide_convert_fusion = bf16[2048,4096]{1,0:T(8,128)(2,1)} fusion(bf16[2048,4096]{1,0:T(8,128)(2,1)} %param.10, f32[2048]{0:T(1024)S(1)} %bitcast.14, bf16[2048,128]{1,0:T(8,128)(2,1)} %param.11, bf16[4096,128]{1,0:T(8,128)(2,1)S(1)} %copy-done), kind=kOutput, calls=%fused_computation | convolution fusion | flops 2222981120 | bytes 35135488 | tf_op jit(solution)/shard_map/dot_general | solution.py:84
  49.8 13.6 %fusion.8 = f32[4096,256]{1,0:T(8,128)} fusion(bf16[2048,4096]{1,0:T(8,128)(2,1)} %divide_convert_fusion, f32[2048]{0:T(1024)S(1)} %copy-done.2, f32[256]{0:T(256)S(1)} %psum.71, f32[2048,256]{1,0:T(8,128)S(1)} %get-tuple-element.15, f32[2048,256]{1,0:T(8,128)} %param.17), kind=kOutput, calls=%fused_computation.24 | convolution fusion | flops 4298113024 | bytes 25175040 | tf_op jit(solution)/shard_map/dot_general | solution.py:95
  63.4 89.7 %all-reduce.5.cloned.1.call-done = f32[4096,256]{1,0:T(8,128)} async-done(((f32[4096,256]{1,0:T(8,128)}), f32[4096,256]{1,0:T(8,128)}) %all-reduce.5.cloned.1.call-update) | async-done | bytes 4194320 | tf_op jit(solution)/shard_map/psum | solution.py:100
  153.2 95.2 %all-reduce.7.cloned.1.call-done = f32[4096,256]{1,0:T(8,128)} async-done(((f32[4096,256]{1,0:T(8,128)}), f32[4096,256]{1,0:T(8,128)}) %all-reduce.7.cloned.1.call-update) | async-done | bytes 4194320 | tf_op jit(solution)/shard_map/psum | solution.py:100
  251.2 9.4 %all_to_all.24 = f32[8,1,512]{2,1,0:T(1,128)S(1)} all-to-all(f32[8,1,512]{2,1,0:T(1,128)S(1)} %broadcast_in_dim.8), channel_id=1, replica_groups=mesh['obl_0'=4,'obl_1'=4,'scn'=8] {'scn'}, dimensions={0} | all-to-all | bytes 32768 | tf_op jit(solution)/shard_map/all_to_all | solution.py:25
  260.7 13.1 %fusion.2 = f32[2048,256]{1,0:T(8,128)} fusion(bf16[2048,4096]{1,0:T(8,128)(2,1)} %divide_convert_fusion, f32[4096,256]{1,0:T(8,128)} %all-reduce.7.cloned.1.call-done, f32[256]{0:T(256)S(1)} %broadcast_multiply_fusion.1, f32[256]{0:T(256)S(1)} %get-tuple-element.12), kind=kOutput, calls=%fused_computation.11 | convolution fusion | flops 4302307328 | bytes 23070720 | tf_op jit(solution)/shard_map/dot_general | solution.py:107
  273.9 31.9 %reduce-scatter.3.cloned.1.call-done = f32[256,256]{1,0:T(8,128)} async-done(((f32[2048,256]{1,0:T(8,128)}), f32[256,256]{1,0:T(8,128)}) %reduce-scatter.3.cloned.1.call-update) | async-done | bytes 262160 | tf_op jit(solution)/shard_map/reduce_scatter | solution.py:51
  305.8 25.5 %all-gather.5.cloned.1.call-done = f32[2048,256]{1,0:T(8,128)} async-done(((f32[256,256]{1,0:T(8,128)}), f32[2048,256]{1,0:T(8,128)}) %all-gather.5.cloned.1.call-update) | async-done | bytes 2097168 | tf_op jit(solution)/shard_map/all_gather | solution.py:54
  335.7 10.4 %psum.74 = f32[256]{0:T(256)S(1)} all-reduce(f32[256]{0:T(256)S(1)} %get-tuple-element.10), channel_id=1, replica_groups=mesh['obl_0'=4,'obl_1'=4,'scn'=8] {'obl_0'}, use_global_device_ids=true, to_apply=%region_10.11 | all-reduce | flops 256 | bytes 2048 | tf_op jit(solution)/shard_map/psum | solution.py:20
  346.1 10.7 %psum.75 = f32[256]{0:T(256)S(1)} all-reduce(f32[256]{0:T(256)S(1)} %psum.74), channel_id=1, replica_groups=mesh['obl_0'=4,'obl_1'=4,'scn'=8] {'obl_1'}, use_global_device_ids=true, to_apply=%region_11.12 | all-reduce | flops 256 | bytes 2048 | tf_op jit(solution)/shard_map/psum | solution.py:20
  356.8 13.6 %fusion.9 = f32[4096,256]{1,0:T(8,128)} fusion(bf16[2048,4096]{1,0:T(8,128)(2,1)} %divide_convert_fusion, f32[2048]{0:T(1024)S(1)} %copy-done.2, f32[2048,256]{1,0:T(8,128)} %get-tuple-element.11, f32[256]{0:T(256)S(1)} %psum.75), kind=kOutput, calls=%fused_computation.25 | convolution fusion | flops 4297588736 | bytes 23077888 | tf_op jit(solution)/shard_map/dot_general | solution.py:95
  370.4 88.8 %all-reduce.9.cloned.1.call-done = f32[4096,256]{1,0:T(8,128)} async-done(((f32[4096,256]{1,0:T(8,128)}), f32[4096,256]{1,0:T(8,128)}) %all-reduce.9.cloned.1.call-update) | async-done | bytes 4194320 | tf_op jit(solution)/shard_map/psum | solution.py:100
  459.5 94.9 %all-reduce.11.cloned.1.call-done = f32[4096,256]{1,0:T(8,128)} async-done(((f32[4096,256]{1,0:T(8,128)}), f32[4096,256]{1,0:T(8,128)}) %all-reduce.11.cloned.1.call-update) | async-done | bytes 4194320 | tf_op jit(solution)/shard_map/psum | solution.py:100
  557.2 9.4 %all_to_all.25 = f32[8,1,512]{2,1,0:T(1,128)S(1)} all-to-all(f32[8,1,512]{2,1,0:T(1,128)S(1)} %broadcast_in_dim.9), channel_id=1, replica_groups=mesh['obl_0'=4,'obl_1'=4,'scn'=8] {'scn'}, dimensions={0} | all-to-all | bytes 32768 | tf_op jit(solution)/shard_map/all_to_all | solution.py:25
  566.6 13.2 %fusion.3 = f32[2048,256]{1,0:T(8,128)} fusion(bf16[2048,4096]{1,0:T(8,128)(2,1)} %divide_convert_fusion, f32[4096,256]{1,0:T(8,128)} %all-reduce.11.cloned.1.call-done, f32[256]{0:T(256)S(1)} %broadcast_multiply_fusion, f32[256]{0:T(256)S(1)} %get-tuple-element.8), kind=kOutput, calls=%fused_computation.12 | convolution fusion | flops 4302307328 | bytes 23070720 | tf_op jit(solution)/shard_map/dot_general | solution.py:107
  579.9 31.9 %reduce-scatter.5.cloned.1.call-done = f32[256,256]{1,0:T(8,128)} async-done(((f32[2048,256]{1,0:T(8,128)}), f32[256,256]{1,0:T(8,128)}) %reduce-scatter.5.cloned.1.call-update) | async-done | bytes 262160 | tf_op jit(solution)/shard_map/reduce_scatter | solution.py:51
  611.8 4.8 fusion
  616.6 7.7 %all_to_all.26 = f32[8,1,256]{2,1,0:T(1,128)S(1)} all-to-all(f32[8,1,256]{2,1,0:T(1,128)S(1)} %broadcast_in_dim.10), channel_id=1, replica_groups=mesh['obl_0'=4,'obl_1'=4,'scn'=8] {'scn'}, dimensions={0} | all-to-all | bytes 16384 | tf_op jit(solution)/shard_map/all_to_all | solution.py:25
  624.3 4.8 fusion.1
  633.0 5.2 all-to-all-done.3
  643.1 10.4 %psum.78 = f32[256]{0:T(256)S(1)} all-reduce(f32[256]{0:T(256)S(1)} %get-tuple-element.6), channel_id=1, replica_groups=mesh['obl_0'=4,'obl_1'=4,'scn'=8] {'obl_0'}, use_global_device_ids=true, to_apply=%region_19.20 | all-reduce | flops 256 | bytes 2048 | tf_op jit(solution)/shard_map/psum | solution.py:20
  653.5 10.8 %psum.79 = f32[256]{0:T(256)S(1)} all-reduce(f32[256]{0:T(256)S(1)} %psum.78), channel_id=1, replica_groups=mesh['obl_0'=4,'obl_1'=4,'scn'=8] {'obl_1'}, use_global_device_ids=true, to_apply=%region_20.21 | all-reduce | flops 256 | bytes 2048 | tf_op jit(solution)/shard_map/psum | solution.py:20
  (52 shorter events, 25.8 us)
Async XLA Ops:
  7.2 26.1 %copy-start = (bf16[4096,128]{1,0:T(8,128)(2,1)S(1)}, bf16[4096,128]{1,0:T(8,128)(2,1)}, u32[]{:S(2)}) copy-start(bf16[4096,128]{1,0:T(8,128)(2,1)} %param.9) | copy-start | bytes 3145732
  7.2 25.3 %copy-start.4 = (f32[16]{0:T(128)S(1)}, f32[16]{0:T(128)}, u32[]{:S(2)}) copy-start(f32[16]{0:T(128)} %param.13) | copy-start | bytes 196
  7.2 25.3 %copy-start.3 = (s32[2048]{0:T(1024)S(1)}, s32[2048]{0:T(1024)}, u32[]{:S(2)}) copy-start(s32[2048]{0:T(1024)} %param.12) | copy-start | bytes 24580
  7.2 145.9 %all-reduce.5.cloned.1.call-start = ((), (), s32[]{:S(2)}) async-start(), calls=%async_computation.6 | async-start | bytes 8388608 | tf_op jit(solution)/shard_map/psum | solution.py:100
  33.2 16.5 %copy-start.2 = (f32[2048]{0:T(1024)S(1)}, f32[2048]{0:T(1024)}, u32[]{:S(2)}) copy-start(f32[2048]{0:T(1024)} %param.14) | copy-start | bytes 24580
  63.4 185.1 %all-reduce.7.cloned.1.call-start = ((), (), s32[]{:S(2)}) async-start(), calls=%async_computation.7 | async-start | bytes 8388608 | tf_op jit(solution)/shard_map/psum | solution.py:100
  153.2 152.6 %reduce-scatter.3.cloned.1.call-start = ((), (), s32[]{:S(2)}) async-start(), calls=%async_computation.8 | async-start | bytes 2359296 | tf_op jit(solution)/shard_map/reduce_scatter | solution.py:51
  273.8 57.5 %all-gather.5.cloned.1.call-start = ((), (), s32[]{:S(2)}) async-start(), calls=%async_computation.12 | async-start | bytes 2359296 | tf_op jit(solution)/shard_map/all_gather | solution.py:54
  305.8 153.4 %all-reduce.9.cloned.1.call-start = ((), (), s32[]{:S(2)}) async-start(), calls=%async_computation.9 | async-start | bytes 8388608 | tf_op jit(solution)/shard_map/psum | solution.py:100
  370.3 184.0 %all-reduce.11.cloned.1.call-start = ((), (), s32[]{:S(2)}) async-start(), calls=%async_computation.10 | async-start | bytes 8388608 | tf_op jit(solution)/shard_map/psum | solution.py:100
  459.2 152.5 %reduce-scatter.5.cloned.1.call-start = ((), (), s32[]{:S(2)}) async-start(), calls=%async_computation.11 | async-start | bytes 2359296 | tf_op jit(solution)/shard_map/reduce_scatter | solution.py:51
  579.9 58.9 %all-gather.7.cloned.1.call-start = ((), (), s32[]{:S(2)}) async-start(), calls=%async_computation.13 | async-start | bytes 2359296 | tf_op jit(solution)/shard_map/all_gather | solution.py:54
  629.7 8.5 %all-to-all-start.3 = ((f32[8,1,256]{2,1,0:T(1,128)}), f32[8,1,256]{2,1,0:T(1,128)S(1)}, u32[]{:S(2)}, u32[]{:S(2)}) async-start(f32[8,1,256]{2,1,0:T(1,128)} %broadcast_in_dim.11), calls=%async_computation.5 | async-start | bytes 16384 | tf_op jit(solution)/shard_map/all_to_all | solution.py:25
  638.8 28.5 %copy-start.1 = (bf16[4096,128]{1,0:T(8,128)(2,1)S(1)}, bf16[4096,128]{1,0:T(8,128)(2,1)}, u32[]{:S(2)}) copy-start(bf16[4096,128]{1,0:T(8,128)(2,1)} %param.9) | copy-start | bytes 3145732
Sparse Core Ops, SparseCore 0:
  63.5 89.6 all-reduce.4
  155.5 92.8 all-reduce.6
  274.0 31.7 reduce-scatter.2
  307.3 23.9 all-gather.4
  370.5 88.7 all-reduce.8
  461.4 92.8 all-reduce.10
  580.0 31.7 reduce-scatter.4
  613.5 24.0 all-gather.6
